TPU v7x, 32 devices: a whole 2x2x4 slice. The times are simulated.
32 devices in a mesh: rep: 1, dp: 32 (over x, y, z, core).
Axes of the slice: x: 2, y: 2, z: 4, core: 2. Of those that a mesh axis runs over, the one named last changes fastest.
Arguments:
- x: bfloat16 [32, 2048, 1024], P(('rep', 'dp'))
- dy: bfloat16 [32, 2048, 1024], P(('rep', 'dp'))
- w_gate: bfloat16 [2, 1024, 2816], replicated
- w_up: bfloat16 [2, 1024, 2816], replicated
- w_down: bfloat16 [2, 2816, 1024], replicated
- m_w_gate: float32 [2, 1024, 2816], replicated
- m_w_up: float32 [2, 1024, 2816], replicated
- m_w_down: float32 [2, 2816, 1024], replicated
- v_w_gate: float32 [2, 1024, 2816], replicated
- v_w_up: float32 [2, 1024, 2816], replicated
- v_w_down: float32 [2, 2816, 1024], replicated
Outputs:
- output 1: bfloat16 [2, 1024, 2816], P('rep')
- output 2: bfloat16 [2, 1024, 2816], P('rep')
- output 3: bfloat16 [2, 2816, 1024], P('rep')
- output 4: float32 [2, 1024, 2816], P('rep')
- output 5: float32 [2, 1024, 2816], P('rep')
- output 6: float32 [2, 2816, 1024], P('rep')
- output 7: float32 [2, 1024, 2816], P('rep')
- output 8: float32 [2, 1024, 2816], P('rep')
- output 9: float32 [2, 2816, 1024], P('rep')
All inputs are finite; a program needn't handle non-finite values.
Results may differ from a plain program's by a relative error of at most 0.022.
Values are sent between devices in bfloat16 or wider.
A program may use at most 2.75 GiB of HBM per device.

v0:
```python
import jax
import jax.numpy as jnp
from jax import lax
from jax.sharding import PartitionSpec as P

NAMES = ("w_gate", "w_up", "w_down")


def matmul(a, w):
    return jnp.dot(a, w, preferred_element_type=jnp.float32).astype(jnp.bfloat16)


def normed(h):
    wide = h.astype(jnp.float32)
    scale = lax.rsqrt(jnp.mean(wide**2, -1, keepdims=True) + 1e-6)
    return (wide * scale).astype(jnp.bfloat16)


def layer(h, w):
    a = normed(h)
    gate = jnp.dot(a, w["w_gate"], preferred_element_type=jnp.float32)
    up = jnp.dot(a, w["w_up"], preferred_element_type=jnp.float32)
    return h + matmul((jax.nn.silu(gate) * up).astype(jnp.bfloat16), w["w_down"])


def adamw(w, m, v, g):
    m = 0.9 * m + 0.1 * g
    v = 0.95 * v + 0.05 * g * g
    step = m * lax.rsqrt(v + 1e-8) + 0.1 * w
    return (w - 0.02 * step).astype(jnp.bfloat16), m, v


def clipped(gradients, sum_of_squares, count):
    factor = jnp.minimum(1.0, 0.5 * lax.rsqrt(sum_of_squares / count + 1e-30))
    return [g * factor for g in gradients]


def solution(mesh):
    def step(x, dy, *arrays):
        weights, m, v = (arrays[i : i + 3] for i in (0, 3, 6))
        layers = weights[0].shape[0]
        h, kept = x[0], []
        for number in range(layers):
            kept.append(h)
            h = layer(h, {name: w[number] for name, w in zip(NAMES, weights, strict=True)})
        by_h, summed = dy[0], [None] * layers
        for number in reversed(range(layers)):
            _, back = jax.vjp(lambda w, h: layer(h, w), {name: w[number] for name, w in zip(NAMES, weights, strict=True)}, kept[number])
            by_w, by_h = back(by_h)
            summed[number] = [lax.psum(by_w[name], "dp") for name in NAMES]
        gradients = [jnp.stack([summed[number][i] for number in range(layers)]).astype(jnp.float32) for i in range(3)]
        gradients = clipped(gradients, sum(jnp.sum(g * g) for g in gradients), sum(g.size for g in gradients))
        new = [adamw(w.astype(jnp.float32), m, v, g) for w, m, v, g in zip(weights, m, v, gradients, strict=True)]
        return tuple(one[which] for which in range(3) for one in new)

    return jax.shard_map(
        step,
        mesh=mesh,
        in_specs=(P(("rep", "dp"), None, None),) * 2 + (P(None, None, None),) * 9,
        out_specs=(P("rep", None, None),) * 9,
        check_vma=False,
    )
```

profile of v0, /device:TPU:0, one launch (start us, length us, event | category | flops | bytes accessed | tf_op | source)
XLA Modules:
  0.0 1033.2 jit_solution(13002271369451718313)
XLA Ops:
  7.2 0.0 all-reduce.3.cloned.1.call-start
  7.2 6.5 copy.20
  13.7 3.1 fusion.36
  16.8 0.0 copy-start.7
  16.8 6.5 copy.21
  23.3 0.0 copy-start.4
  23.3 18.3 %convolution_convert_fusion.1 = bf16[2048,2816]{1,0:T(8,128)(2,1)} fusion(bf16[2,2816,1024]{2,1,0:T(8,128)(2,1)} %param.15, bf16[1,2048,1024]{2,1,0:T(8,128)(2,1)} %param.12), kind=kOutput, calls=%fused_computation.68 | convolution fusion | flops 11816927232 | bytes 21495808 | tf_op jit(solution)/shard_map/transpose(jvp())/dot_general | solution.py:10
  41.6 0.0 copy-done.4
  41.6 18.3 %fusion.56 = f32[2048,2816]{1,0:T(8,128)} fusion(bf16[2,1024,2816]{2,1,0:T(8,128)(2,1)} %param.13, bf16[1,2048,1024]{2,1,0:T(8,128)(2,1)S(1)} %copy-done.4, f32[2048]{0:T(1024)S(1)} %add_rsqrt_fusion), kind=kOutput, calls=%fused_computation.93 | convolution fusion | flops 11817451520 | bytes 33038336 | tf_op jit(solution)/shard_map/dot_general | solution.py:21
  59.9 0.0 copy-done.7
  59.9 28.7 %multiply_convert_fusion.1 = (bf16[2048,2816]{1,0:T(8,128)(2,1)}, f32[2048,2816]{1,0:T(8,128)}) fusion(f32[2048,2816]{1,0:T(8,128)} %fusion.56, bf16[2,1024,2816]{2,1,0:T(8,128)(2,1)} %param.14, bf16[1,2048,1024]{2,1,0:T(8,128)(2,1)} %param.11, f32[2048]{0:T(1024)S(1)} %add_rsqrt_fusion), kind=kOutput, calls=%fused_computation.53 | convolution fusion | flops 11852054528 | bytes 67641344 | tf_op jit(solution)/shard_map/dot_general | solution.py:22
  88.6 19.8 %fusion.40 = (f32[2048]{0:T(1024)S(1)}, bf16[2048,1024]{0,1:T(8,128)(2,1)}) fusion(bf16[2048,2816]{1,0:T(8,128)(2,1)} %get-tuple-element.24, bf16[2,2816,1024]{2,1,0:T(8,128)(2,1)} %param.15, bf16[1,2048,1024]{1,2,0:T(8,128)(2,1)} %copy.20), kind=kOutput, calls=%fused_computation.76 | convolution fusion | flops 11821643776 | bytes 25698304 | tf_op jit(solution)/shard_map/dot_general | solution.py:10
  108.4 0.6 copy-done.5
  109.0 0.0 copy-start.1
  109.0 20.3 %fusion.43 = f32[2048,2816]{1,0:T(8,128)} fusion(bf16[2,1024,2816]{2,1,0:T(8,128)(2,1)} %param.14, bf16[2048,1024]{0,1:T(8,128)(2,1)} %get-tuple-element.27, f32[2048]{0:T(1024)S(1)} %fusion.86), kind=kOutput, calls=%fused_computation.80 | convolution fusion | flops 11817451520 | bytes 33038336 | tf_op jit(solution)/shard_map/jvp()/dot_general | solution.py:22
  129.3 0.0 copy-done.1
  129.3 31.5 %fusion.20 = (bf16[2048,2816]{1,0:T(8,128)(2,1)}, f32[2048,2816]{1,0:T(8,128)}) fusion(f32[2048,2816]{1,0:T(8,128)} %fusion.43, bf16[2048,2816]{1,0:T(8,128)(2,1)} %convolution_convert_fusion.1, bf16[2,1024,2816]{2,1,0:T(8,128)(2,1)} %param.13, bf16[2048,1024]{0,1:T(8,128)(2,1)S(1)} %copy-done.1, f32[2048]{0:T(1024)S(1)} %fusion.86), kind=kOutput, calls=%fused_computation.41 | convolution fusion | flops 11886657536 | bytes 79175680 | tf_op jit(solution)/shard_map/jvp()/dot_general | solution.py:21
  160.8 20.2 %fusion.33 = bf16[2048,1024]{0,1:T(8,128)(2,1)} fusion(bf16[2048,2816]{1,0:T(8,128)(2,1)} %convolution_convert_fusion.1, bf16[2,1024,2816]{2,1,0:T(8,128)(2,1)} %param.14, f32[2048,2816]{1,0:T(8,128)} %get-tuple-element.29), kind=kOutput, calls=%fused_computation.57 | convolution fusion | flops 11845763072 | bytes 44564480 | tf_op jit(solution)/shard_map/transpose(jvp())/dot_general | solution.py:22
  181.0 22.4 %convert_bitcast_fusion.2 = bf16[1,1024,2816]{2,1,0:T(8,128)(2,1)} fusion(bf16[2048,2816]{1,0:T(8,128)(2,1)} %convolution_convert_fusion.1, bf16[2048,1024]{0,1:T(8,128)(2,1)} %get-tuple-element.27, f32[2048]{0:T(1024)S(1)} %fusion.86, f32[2048,2816]{1,0:T(8,128)} %get-tuple-element.29), kind=kOutput, calls=%fused_computation.97 | convolution fusion | flops 11854938112 | bytes 44572672 | tf_op jit(solution)/shard_map/transpose(jvp())/dot_general | solution.py:22
  203.4 0.0 copy-start.2
  203.4 23.8 %convert_bitcast_fusion = bf16[1,2816,1024]{2,1,0:T(8,128)(2,1)} fusion(f32[2048,2816]{1,0:T(8,128)} %fusion.43, bf16[1,2048,1024]{2,1,0:T(8,128)(2,1)} %param.12, f32[2048,2816]{1,0:T(8,128)} %get-tuple-element.29), kind=kOutput, calls=%fused_computation.95 | convolution fusion | flops 11848646656 | bytes 56098816 | tf_op jit(solution)/shard_map/transpose(jvp())/dot_general | solution.py:10
  227.1 0.0 copy-done.2
  227.1 17.5 %convert_bitcast_fusion.4 = bf16[1,1024,2816]{2,1,0:T(8,128)(2,1)} fusion(bf16[2048,2816]{1,0:T(8,128)(2,1)} %get-tuple-element.28, bf16[2048,1024]{0,1:T(8,128)(2,1)S(1)} %copy-done.2, f32[2048]{0:T(1024)S(1)} %fusion.86), kind=kOutput, calls=%fused_computation.99 | convolution fusion | flops 11817451520 | bytes 21504000 | tf_op jit(solution)/shard_map/transpose(jvp())/dot_general | solution.py:21
  244.7 0.0 copy-start.6
  244.7 0.0 copy-start
  244.7 19.6 %fusion.42 = (f32[2048]{0:T(1024)S(1)}, bf16[2048,1024]{0,1:T(8,128)(2,1)}) fusion(bf16[2048,1024]{0,1:T(8,128)(2,1)S(1)} %copy-done.2, bf16[2048,1024]{0,1:T(8,128)(2,1)} %fusion.33, bf16[2048,2816]{1,0:T(8,128)(2,1)} %get-tuple-element.28, bf16[2,1024,2816]{2,1,0:T(8,128)(2,1)} %param.13), kind=kOutput, calls=%fused_computation.78 | convolution fusion | flops 11821643776 | bytes 29892608 | tf_op jit(solution)/shard_map/transpose(jvp())/dot_general | solution.py:21
  264.3 0.0 copy-done.6
  264.3 0.0 copy-done
  264.4 6.0 fusion.70
  270.4 18.4 %convolution_convert_fusion = bf16[2048,2816]{1,0:T(8,128)(2,1)} fusion(bf16[2048,1024]{0,1:T(8,128)(2,1)} %fusion.70, bf16[2,2816,1024]{2,1,0:T(8,128)(2,1)} %param.15), kind=kOutput, calls=%fused_computation.67 | convolution fusion | flops 11816927232 | bytes 21495808 | tf_op jit(solution)/shard_map/transpose(jvp())/dot_general | solution.py:10
  288.8 0.0 copy-done.3
  288.8 17.0 %convert_bitcast_fusion.1 = bf16[1,2816,1024]{2,1,0:T(8,128)(2,1)} fusion(bf16[2048,2816]{1,0:T(8,128)(2,1)} %get-tuple-element.24, bf16[2048,1024]{0,1:T(8,128)(2,1)S(1)} %copy-done.3), kind=kOutput, calls=%fused_computation.96 | convolution fusion | flops 11814043648 | bytes 21495808 | tf_op jit(solution)/shard_map/transpose(jvp())/dot_general | solution.py:10
  305.8 0.0 copy-done.8
  305.8 22.3 %convert_bitcast_fusion.3 = bf16[1,1024,2816]{2,1,0:T(8,128)(2,1)} fusion(bf16[2048,2816]{1,0:T(8,128)(2,1)} %convolution_convert_fusion, f32[2048,2816]{1,0:T(8,128)} %fusion.56, bf16[1,2048,1024]{1,2,0:T(8,128)(2,1)} %copy.20, f32[2048]{0:T(1024)S(1)} %copy-done.8), kind=kOutput, calls=%fused_computation.98 | convolution fusion | flops 11854938112 | bytes 44572672 | tf_op jit(solution)/shard_map/transpose(jvp())/dot_general | solution.py:22
  328.1 26.9 %convert_bitcast_fusion.5 = bf16[1,1024,2816]{2,1,0:T(8,128)(2,1)} fusion(f32[2048,2816]{1,0:T(8,128)} %fusion.56, f32[2048,2816]{1,0:T(8,128)} %get-tuple-element.25, bf16[2048,2816]{1,0:T(8,128)(2,1)} %convolution_convert_fusion, bf16[1,2048,1024]{1,2,0:T(8,128)(2,1)} %copy.20, f32[2048]{0:T(1024)S(1)} %copy-done.8), kind=kOutput, calls=%fused_computation.100 | convolution fusion | flops 11883773952 | bytes 67641344 | tf_op jit(solution)/shard_map/transpose(jvp())/dot_general | solution.py:21
  355.0 0.0 all-reduce.3.cloned.1.call-update
  355.0 513.9 %all-reduce.3.cloned.1.call-done = (bf16[1,1024,2816]{2,1,0:T(8,128)(2,1)}, bf16[1,1024,2816]{2,1,0:T(8,128)(2,1)}, bf16[1,1024,2816]{2,1,0:T(8,128)(2,1)}, bf16...) async-done(((bf16[1,1024,2816]{2,1,0:T(8,128)(2,1)}, bf16[1,1024,2816]{2,1,0:T(8,128)(2,1)}, ...) | async-done | bytes 34603024 | tf_op jit(solution)/shard_map/psum | solution.py:50
  869.0 11.0 %fusion.10 = f32[]{:T(128)} fusion(bf16[1,1024,2816]{2,1,0:T(8,128)(2,1)} %get-tuple-element.9, bf16[1,1024,2816]{2,1,0:T(8,128)(2,1)} %get-tuple-element.10), kind=kLoop, calls=%fused_computation.31 | loop fusion | flops 23068672 | bytes 11534340 | tf_op jit(solution)/shard_map/reduce_sum | solution.py:52
  880.0 0.0 slice-done.2
  880.0 0.0 slice-done.3
  880.0 9.2 fusion.11
  890.5 0.0 slice-start
  890.5 11.2 %fusion.12 = f32[]{:T(128)} fusion(bf16[1,2816,1024]{2,1,0:T(8,128)(2,1)} %get-tuple-element.13, bf16[1,2816,1024]{2,1,0:T(8,128)(2,1)} %get-tuple-element.14), kind=kLoop, calls=%fused_computation.33 | loop fusion | flops 23068672 | bytes 11534340 | tf_op jit(solution)/shard_map/reduce_sum | solution.py:52
  902.4 0.0 slice-start.1
  902.4 40.7 %fusion.18 = (bf16[2,2816,1024]{2,1,0:T(8,128)(2,1)}, f32[2,2816,1024]{2,1,0:T(8,128)}, f32[2,2816,1024]{2,1,0:T(8,128)}) fusion(bf16[2,2816,1024]{2,1,0:T(8,128)(2,1)} %param.15, f32[]{:T(128)S(6)} %min_shard_map.3, bf16[1,2816,1024]{2,1,0:T(8,128)(2,1)} %get-tuple-element.13, bf16[1,2816,1024]{2,1,0:T(8,128)(2,1)} %get-tuple-element.14, ...), kind=kLoop, calls=%fused_computation.39 | loop fusion | flops 115343360 | bytes 126877696 | tf_op jit(solution)/shard_map/convert_element_type | solution.py:30
  943.1 0.0 slice-done
  943.1 0.0 slice-done.1
  943.1 82.7 %fusion.8 = (bf16[2,1024,2816]{2,1,0:T(8,128)(2,1)}, f32[2,1024,2816]{2,1,0:T(8,128)}, f32[2,1024,2816]{2,1,0:T(8,128)}, bf16[2,1024,2816]{2,1,0:T(8,128)(2,1)},...) fusion(bf16[2,1024,2816]{2,1,0:T(8,128)(2,1)} %param.13, f32[]{:T(128)S(6)} %min_shard_map.3, ...), kind=kLoop, calls=%fused_computation.29 | loop fusion | flops 230686720 | bytes 253755392 | tf_op jit(solution)/shard_map/convert_element_type | solution.py:30
  (10 shorter events, 0.0 us)
Async XLA Ops:
  7.2 861.8 %all-reduce.3.cloned.1.call-start = ((), (), s32[]{:S(2)}) async-start(), calls=%async_computation | async-start | bytes 69206016 | tf_op jit(solution)/shard_map/psum | solution.py:50
  16.8 43.1 %copy-start.7 = (f32[2048]{0:T(1024)}, f32[2048]{0:T(1024)S(1)}, u32[]{:S(2)}) copy-start(f32[2048]{0:T(1024)S(1)} %add_rsqrt_fusion) | copy-start | bytes 24580
  23.3 18.3 %copy-start.4 = (bf16[1,2048,1024]{2,1,0:T(8,128)(2,1)S(1)}, bf16[1,2048,1024]{2,1,0:T(8,128)(2,1)}, u32[]{:S(2)}) copy-start(bf16[1,2048,1024]{2,1,0:T(8,128)(2,1)} %param.11) | copy-start | bytes 12582916
  108.4 0.6 copy-start.5
  109.0 20.3 %copy-start.1 = (bf16[2048,1024]{0,1:T(8,128)(2,1)S(1)}, bf16[2048,1024]{0,1:T(8,128)(2,1)}, u32[]{:S(2)}) copy-start(bf16[2048,1024]{0,1:T(8,128)(2,1)} %get-tuple-element.27) | copy-start | bytes 12582916
  203.4 23.8 %copy-start.2 = (bf16[2048,1024]{0,1:T(8,128)(2,1)S(1)}, bf16[2048,1024]{0,1:T(8,128)(2,1)}, u32[]{:S(2)}) copy-start(bf16[2048,1024]{0,1:T(8,128)(2,1)} %get-tuple-element.27) | copy-start | bytes 12582916
  244.7 19.6 %copy-start.6 = (f32[2048]{0:T(1024)S(1)}, f32[2048]{0:T(1024)}, u32[]{:S(2)}) copy-start(f32[2048]{0:T(1024)} %copy-done.5) | copy-start | bytes 24580
  244.7 19.7 %copy-start = (bf16[1,2048,1024]{1,2,0:T(8,128)(2,1)S(1)}, bf16[1,2048,1024]{1,2,0:T(8,128)(2,1)}, u32[]{:S(2)}) copy-start(bf16[1,2048,1024]{1,2,0:T(8,128)(2,1)} %copy.21) | copy-start | bytes 12582916
  270.4 18.4 %copy-start.3 = (bf16[2048,1024]{0,1:T(8,128)(2,1)S(1)}, bf16[2048,1024]{0,1:T(8,128)(2,1)}, u32[]{:S(2)}) copy-start(bf16[2048,1024]{0,1:T(8,128)(2,1)} %fusion.70) | copy-start | bytes 12582916
  288.8 17.0 %copy-start.8 = (f32[2048]{0:T(1024)S(1)}, f32[2048]{0:T(1024)}, u32[]{:S(2)}) copy-start(f32[2048]{0:T(1024)} %copy-done.7) | copy-start | bytes 24580
  869.0 11.0 %slice-start.2 = ((s8[5767168]{0:T(1024)(128)(4,1)}), s8[4194304]{0:T(1024)(128)(4,1)S(1)}, s32[]{:S(2)}) async-start(s8[5767168]{0:T(1024)(128)(4,1)} %bitcast.76), calls=%async_computation.3 | async-start | bytes 8388608
  869.0 11.0 %slice-start.3 = ((s8[5767168]{0:T(1024)(128)(4,1)}), s8[1572864]{0:T(1024)(128)(4,1)S(1)}, s32[]{:S(2)}) async-start(s8[5767168]{0:T(1024)(128)(4,1)} %bitcast.76), calls=%async_computation.4 | async-start | bytes 3145728
  890.5 52.7 %slice-start = ((s8[5767168]{0:T(1024)(128)(4,1)}), s8[1572864]{0:T(1024)(128)(4,1)S(1)}, s32[]{:S(2)}) async-start(s8[5767168]{0:T(1024)(128)(4,1)} %bitcast.74), calls=%async_computation.1 | async-start | bytes 3145728
  902.4 40.7 %slice-start.1 = ((s8[5767168]{0:T(1024)(128)(4,1)}), s8[4194304]{0:T(1024)(128)(4,1)S(1)}, s32[]{:S(2)}) async-start(s8[5767168]{0:T(1024)(128)(4,1)} %bitcast.74), calls=%async_computation.2 | async-start | bytes 8388608
Sparse Core Ops, SparseCore 0:
  355.2 513.7 all-reduce.2
where the time goes:
time: 1040 us; the launch traced here: 1030 us
  waiting for transfers between devices  514 us (49%)
  matrix products  325 us (31%)
  other arithmetic  164 us (16%)
  between operations  16.6 us (2%)
  local copies, waits for them, and re-layouts  13.7 us (1%)
    psum x1, waiting for transfers between devices, step(): summed[number] = [lax.psum(by_w[name], 'dp') for name in NAMES]  514 us
    convert_element_type x2, other arithmetic, adamw(): return ((w - 0.02 * step).astype(jnp.bfloat16), m, v)  123 us
    dot_general x5, matrix products, layer(): up = jnp.dot(a, w['w_up'], preferred_element_type=jnp.float32)  114 us
    dot_general x5, matrix products, layer(): gate = jnp.dot(a, w['w_gate'], preferred_element_type=jnp.float32)  114 us
    dot_general x5, matrix products, matmul(): jnp.dot(a, w, preferred_element_type=jnp.float32).astype(jnp.bfloat16)  97.2 us
    reduce_sum x3, other arithmetic, step(): jnp.sum(g * g)  31.4 us
  transfers between devices with their start and end apart: 1, of which 1 were waited for; matrix products, arithmetic and copies ran while one was open for 0% of the time, Pallas kernels for 0%

commit v1 on v0

v1 whole, which is shorter than its diff:
```python
import functools

import jax
import jax.numpy as jnp
from jax import lax
from jax.experimental import pallas as pl
from jax.experimental.pallas import tpu as pltpu
from jax.sharding import PartitionSpec as P

BF, F32 = jnp.bfloat16, jnp.float32
MiB = 2**20
ROWS = 256
CH = 256
STAGES = 4
ANY = pl.BlockSpec(memory_space=pl.ANY)
VMEM = pl.BlockSpec(memory_space=pltpu.VMEM)


def nn(a, b):
    return jnp.dot(a, b, preferred_element_type=F32)


def nt(a, b):
    return lax.dot_general(a, b, (((1,), (1,)), ((), ())), preferred_element_type=F32)


def normed(h):
    wide = h.astype(F32)
    scale = lax.rsqrt(jnp.mean(wide * wide, -1, keepdims=True) + 1e-6)
    return (wide * scale).astype(BF)


def gated(gate, up):
    sig = lax.logistic(gate)
    act = gate * sig
    return act * up, up * (sig + act * (1.0 - sig)), act


def weights_in(refs, bufs, sem):
    first = pl.program_id(0) == 0
    copies = [pltpu.make_async_copy(r, b, sem.at[i]) for i, (r, b) in enumerate(zip(refs, bufs, strict=True))]

    @pl.when(first)
    def _():
        for c in copies:
            c.start()

    def wait(i):
        @pl.when(first)
        def _():
            copies[i].wait()

    return wait


def forward_kernel(layer, x_ref, wg_hbm, wu_hbm, wd_hbm, s_ref, fa_ref, fb_ref, at_ref, h_ref, wg, wu, wd, sem):
    wait = weights_in([r.at[layer] for r in (wg_hbm, wu_hbm, wd_hbm)], (wg, wu, wd), sem)
    x = x_ref[0]
    a = normed(x)
    at_ref[...] = a.T
    wait(0)
    wait(1)
    for c in range(0, wg.shape[1], CH):
        cols = pl.ds(c, CH)
        prod, slope_g, slope_u = gated(nn(a, wg[:, cols]), nn(a, wu[:, cols]))
        s_ref[:, cols] = prod.astype(BF)
        fa_ref[:, cols] = slope_g
        fb_ref[:, cols] = slope_u
    wait(2)
    out = nn(s_ref[...], wd[...]).astype(BF)
    h_ref[...] = (x.astype(F32) + out.astype(F32)).astype(BF)


def top_kernel(layer, h_ref, dy_ref, wg_hbm, wu_hbm, wd_hbm, s_ref, dg_ref, du_ref, at_ref, dyt_ref, wg, wu, wd, sem):
    wait = weights_in([r.at[layer] for r in (wg_hbm, wu_hbm, wd_hbm)], (wg, wu, wd), sem)
    a = normed(h_ref[...])
    dy = dy_ref[0]
    at_ref[...] = a.T
    dyt_ref[...] = dy.T
    for i in range(3):
        wait(i)
    for c in range(0, wg.shape[1], CH):
        cols = pl.ds(c, CH)
        prod, slope_g, slope_u = gated(nn(a, wg[:, cols]), nn(a, wu[:, cols]))
        s_ref[:, cols] = prod.astype(BF)
        ds = nt(dy, wd[cols, :]).astype(BF).astype(F32)
        dg_ref[:, cols] = (ds * slope_g).astype(BF)
        du_ref[:, cols] = (ds * slope_u).astype(BF)


def between_kernel(layer, dg1_ref, du1_ref, h_ref, dy_ref, fa_ref, fb_ref, wg_hbm, wu_hbm, wd_hbm, dg_ref, du_ref, dht_ref, wg, wu, wd, sem):
    wait = weights_in([wg_hbm.at[layer + 1], wu_hbm.at[layer + 1], wd_hbm.at[layer]], (wg, wu, wd), sem)
    wait(0)
    by_gate = nt(dg1_ref[...], wg[...]).astype(BF).astype(F32)
    wait(1)
    by_up = nt(du1_ref[...], wu[...]).astype(BF).astype(F32)
    da = (by_gate + by_up).astype(BF).astype(F32)
    wide = h_ref[...].astype(F32)
    scale = lax.rsqrt(jnp.mean(wide * wide, -1, keepdims=True) + 1e-6)
    inner = jnp.mean(da * wide, -1, keepdims=True)
    dn = (da * scale - wide * (scale * scale * scale * inner)).astype(BF)
    dh = (dy_ref[0].astype(F32) + dn.astype(F32)).astype(BF)
    dht_ref[...] = dh.T
    wait(2)
    for c in range(0, wd.shape[0], CH):
        cols = pl.ds(c, CH)
        ds = nt(dh, wd[cols, :]).astype(BF).astype(F32)
        dg_ref[:, cols] = (ds * fa_ref[:, cols]).astype(BF)
        du_ref[:, cols] = (ds * fb_ref[:, cols]).astype(BF)


def row_local(kernel, name, ins, weights, outs, matmuls):
    tokens, d, ff = 2048, weights[0].shape[1], weights[0].shape[2]

    def spec(a):
        if len(a.shape) == 3:
            return pl.BlockSpec((1, ROWS, a.shape[2]), lambda i: (0, i, 0))
        if a.shape[1] == tokens:
            return pl.BlockSpec((a.shape[0], ROWS), lambda i: (0, i))
        return pl.BlockSpec((ROWS, a.shape[1]), lambda i: (i, 0))

    return pl.pallas_call(
        kernel,
        grid=(tokens // ROWS,),
        in_specs=[spec(a) for a in ins] + [ANY] * 3,
        out_specs=[spec(a) for a in outs],
        out_shape=outs,
        scratch_shapes=[pltpu.VMEM((d, ff), BF), pltpu.VMEM((d, ff), BF), pltpu.VMEM((ff, d), BF), pltpu.SemaphoreType.DMA((3,))],
        compiler_params=pltpu.CompilerParams(dimension_semantics=("arbitrary",), vmem_limit_bytes=62 * MiB),
        cost_estimate=pl.CostEstimate(flops=matmuls * 2 * tokens * d * ff, bytes_accessed=8 * tokens * ff, transcendentals=0),
        name=name,
    )(*ins, *weights)


def struct(dtype, *shape):
    return jax.ShapeDtypeStruct(shape, dtype)


def colour(c):
    late = c % 9
    along_z = (late == 4) | (late == 8)
    return jnp.where(along_z, 2, c % 2)


def bit_of(stage, c):
    if stage == 0:
        return 1
    k = colour(c)
    x, y, z = ((16, 8, 2, 4)[stage - 1], (8, 16, 2, 4)[stage - 1], (2, 4, 16, 8)[stage - 1])
    return jnp.where(k == 2, z, jnp.where(k == 0, x, y))


def side_of(me, bit):
    return (me // bit) % 2


def partner_of(me, bit):
    return me + bit - 2 * bit * side_of(me, bit)


def rows_of(device, c):
    at = side_of(device, 1) * 512
    for k in range(1, STAGES + 1):
        at = at + side_of(device, bit_of(k, c)) * (512 >> k)
    return at


def mult(x, m):
    return pl.multiple_of(x, m)


def reduce_kernel(n, per, lags, lhs_d, lhs_g, s_ref, dg_ref, du_ref, own_ref, sq_ref,
                  lhs, rhs, acc, send0, recv0, bufs_s, bufs_r, lhs_sem, rhs_sem, ssem0, rsem0, ssem, rsem):
    me = lax.axis_index("dp")
    total = 3 * per
    half = 512
    core = side_of(me, 1)

    def rhs_start(c):
        for which, ref in enumerate((s_ref, dg_ref, du_ref)):
            @pl.when((c >= which * per) & (c < (which + 1) * per))
            def _():
                cols = pl.ds(mult((c - which * per) * CH, CH), CH)
                pltpu.make_async_copy(ref.at[:, cols], rhs.at[c % 3], rhs_sem.at[c % 3]).start()

    def rhs_wait(c):
        pltpu.make_async_copy(s_ref.at[:, pl.ds(0, CH)], rhs.at[c % 3], rhs_sem.at[c % 3]).wait()

    def core_copy(c):
        return pltpu.make_async_remote_copy(send0.at[c % 4], recv0.at[c], ssem0.at[c % 4], rsem0.at[c],
                                            device_id={"dp": partner_of(me, 1)}, device_id_type=pl.DeviceIdType.MESH)

    def stage_copy(k, c):
        return pltpu.make_async_remote_copy(bufs_s[k - 1].at[c], bufs_r[k - 1].at[c], ssem.at[k - 1, c], rsem.at[k - 1, c],
                                            device_id={"dp": partner_of(me, bit_of(k, c))}, device_id_type=pl.DeviceIdType.MESH)

    cps = [pltpu.make_async_copy(lhs_d, lhs.at[0], lhs_sem.at[0]), pltpu.make_async_copy(lhs_g, lhs.at[1], lhs_sem.at[1])]
    cps[0].start()
    rhs_start(0)
    rhs_start(1)
    cps[1].start()
    cps[0].wait()
    cps[1].wait()
    sq_ref[...] = jnp.zeros_like(sq_ref)

    def compute(c):
        rhs_wait(c)
        @pl.when(c + 2 < total)
        def _():
            rhs_start(c + 2)
        @pl.when(c >= 4)
        def _():
            core_copy(c - 4).wait_send()
        which = jnp.where(c < per, 0, 1)
        b = rhs[c % 3]
        send0[c % 4] = jnp.dot(lhs[which, pl.ds(mult((1 - core) * half, half), half), :], b, preferred_element_type=F32).astype(BF)
        acc[c] = jnp.dot(lhs[which, pl.ds(mult(core * half, half), half), :], b, preferred_element_type=F32)
        core_copy(c).start()

    def offset(k, c):
        at = 0
        for s in range(1, k + 1):
            at = at + side_of(me, bit_of(s, c)) * (half >> s)
        return at

    def stage_job(k, c):
        if k == 0:
            core_copy(c).wait_recv()
            got = recv0
        else:
            stage_copy(k, c).wait_recv()
            got = bufs_r[k - 1]
        base = offset(k, c)
        rows = half >> k
        if k == STAGES:
            out = (acc[c, pl.ds(mult(base, rows), rows), :] + got[c].astype(F32)).astype(BF)
            own_ref[c] = out
            wide = out.astype(F32)
            sq_ref[...] += wide * wide
            return
        n2 = rows // 2
        side = side_of(me, bit_of(k + 1, c))
        ds, dk = mult((1 - side) * n2, n2), mult(side * n2, n2)
        bufs_s[k][c] = (acc[c, pl.ds(mult(base + ds, n2), n2), :] + got[c, pl.ds(ds, n2), :].astype(F32)).astype(BF)
        stage_copy(k + 1, c).start()
        acc[c, pl.ds(mult(base + dk, n2), n2), :] += got[c, pl.ds(dk, n2), :].astype(F32)

    lag0, *later = lags
    steps = total + later[-1]

    def step(i, _):
        @pl.when(i < total)
        def _():
            compute(i)
        @pl.when((i >= lag0) & (i < total + lag0))
        def _():
            stage_job(0, i - lag0)
        for k in range(1, STAGES + 1):
            c = i - later[k - 1]
            @pl.when((c >= 0) & (c < total))
            def _():
                stage_job(k, c)
        return 0

    lax.fori_loop(0, steps, step, 0)

    def settle(c, _):
        for k in range(1, STAGES + 1):
            stage_copy(k, c).wait_send()
        return 0

    lax.fori_loop(0, total, settle, 0)
    for c in range(total - 4, total):
        core_copy(c).wait_send()


def entry(fn):
    def wrapped(*refs):
        me = lax.axis_index("dp")
        barrier = pltpu.get_barrier_semaphore()
        for bit in (1, 2, 4, 8, 16):
            pl.semaphore_signal(barrier, inc=1, device_id={"dp": partner_of(me, bit)}, device_id_type=pl.DeviceIdType.MESH)
        pl.semaphore_wait(barrier, 5)
        fn(*refs)
    return wrapped


def reduced(lhs_d, lhs_g, s, dg, du, cid, lags=(2, 6, 10, 14, 18)):
    n = 32
    per = s.shape[1] // CH
    total = 3 * per
    T = s.shape[0]

    def body(a, b, c, d, e, own, sq, lhs, rhs, acc, send0, recv0, s1, s2, s3, s4, r1, r2, r3, r4, *sems):
        reduce_kernel(n, per, lags, a, b, c, d, e, own, sq, lhs, rhs, acc, send0, recv0, (s1, s2, s3, s4), (r1, r2, r3, r4), *sems)

    return pl.pallas_call(
        entry(body),
        out_shape=(jax.ShapeDtypeStruct((total, 32, CH), BF), jax.ShapeDtypeStruct((32, CH), F32)),
        in_specs=[ANY] * 5,
        out_specs=(VMEM, VMEM),
        scratch_shapes=[
            pltpu.VMEM((2, 1024, T), BF),
            pltpu.VMEM((3, T, CH), BF),
            pltpu.VMEM((total, 512, CH), F32),
            pltpu.VMEM((4, 512, CH), BF),
            pltpu.VMEM((total, 512, CH), BF),
            *[pltpu.VMEM((total, 512 >> k, CH), BF) for k in range(1, STAGES + 1)] * 2,
            pltpu.SemaphoreType.DMA((2,)),
            pltpu.SemaphoreType.DMA((3,)),
            pltpu.SemaphoreType.DMA((4,)),
            pltpu.SemaphoreType.DMA((total,)),
            pltpu.SemaphoreType.DMA((STAGES, total)),
            pltpu.SemaphoreType.DMA((STAGES, total)),
        ],
        compiler_params=pltpu.CompilerParams(collective_id=cid, has_side_effects=True, vmem_limit_bytes=63 * MiB),
        cost_estimate=pl.CostEstimate(flops=3 * 2 * T * 1024 * s.shape[1], bytes_accessed=3 * 2 * T * s.shape[1], transcendentals=0),
        name=f"reduce{cid}",
    )(lhs_d, lhs_g, s, dg, du)


def adam_kernel(layer, matrix, per, flip, factor_ref, g_ref, w_ref, m_ref, v_ref, *rest):
    *_, wo_ref, mo_ref, vo_ref, gt = rest
    c = matrix * per + pl.program_id(0)
    factor = factor_ref[0, 0]

    def update(at, g):
        g = g * factor
        m = 0.9 * m_ref[at] + 0.1 * g
        v = 0.95 * v_ref[at] + 0.05 * g * g
        w = w_ref[at].astype(F32)
        wo_ref[at] = (w - 0.02 * (m * lax.rsqrt(v + 1e-8) + 0.1 * w)).astype(BF)
        mo_ref[at] = m
        vo_ref[at] = v

    for device in range(32):
        base = rows_of(device, c)
        if flip:
            gt[pl.ds(mult(base, 32), 32), :] = g_ref[device, 0].astype(F32)
        else:
            update((0, pl.ds(mult(base, 32), 32), slice(None)), g_ref[device, 0].astype(F32))
    if flip:
        for q in range(0, 1024, 128):
            update((0, slice(None), pl.ds(q, 128)), gt[pl.ds(q, 128), :].T)


def adam(layer, matrix, flip, factor, g, w, m, v, before):
    layers, rows, columns = w.shape
    per = (rows if flip else columns) // CH
    if flip:
        block = pl.BlockSpec((1, CH, columns), lambda j: (layer, j, 0))
    else:
        block = pl.BlockSpec((1, rows, CH), lambda j: (layer, 0, j))
    before = before or ()
    return pl.pallas_call(
        functools.partial(adam_kernel, layer, matrix, per, flip),
        grid=(per,),
        in_specs=[
            pl.BlockSpec(memory_space=pltpu.SMEM),
            pl.BlockSpec((32, 1, 32, CH), lambda j: (0, matrix * per + j, 0, 0)),
            block, block, block, *[ANY] * len(before),
        ],
        out_specs=[block] * 3,
        out_shape=(struct(BF, *w.shape), struct(F32, *w.shape), struct(F32, *w.shape)),
        scratch_shapes=[pltpu.VMEM((1024, CH), F32)],
        input_output_aliases={5 + i: i for i in range(len(before))},
        compiler_params=pltpu.CompilerParams(dimension_semantics=("arbitrary",), vmem_limit_bytes=48 * MiB),
        cost_estimate=pl.CostEstimate(flops=10 * rows * columns, bytes_accessed=22 * rows * columns, transcendentals=rows * columns),
        name=f"adam{layer}{matrix}",
    )(factor, g, w, m, v, *before)


def solution(mesh):
    def step(x, dy, *arrays):
        weights, m, v = (arrays[i : i + 3] for i in (0, 3, 6))
        layers, d, ff = weights[0].shape
        t = x.shape[1]
        wide, tall, flat = struct(BF, t, ff), struct(BF, d, t), struct(BF, t, d)
        s0, fa, fb, a0t, h1 = row_local(functools.partial(forward_kernel, 0), "fwd0", [x], weights,
                                        [wide, struct(F32, t, ff), struct(F32, t, ff), tall, flat], 3)
        s1, dg1, du1, a1t, dyt = row_local(functools.partial(top_kernel, 1), "top", [h1, dy], weights, [wide, wide, wide, tall, tall], 3)
        own1, sq1 = reduced(dyt, a1t, s1, dg1, du1, 1)
        dg0, du0, dht = row_local(functools.partial(between_kernel, 0), "between", [dg1, du1, h1, dy, fa, fb], weights, [wide, wide, tall], 3)
        own0, sq0 = reduced(dht, a0t, s0, dg0, du0, 2)
        squares = lax.psum(jnp.sum(sq1) + jnp.sum(sq0), "dp")
        count = 3 * layers * d * ff
        factor = jnp.minimum(1.0, 0.5 * lax.rsqrt(squares / count + 1e-30)).reshape(1, 1)
        g1 = lax.all_gather(own1, "dp")
        g0 = lax.all_gather(own0, "dp")
        new = {}
        for name, which, matrix, flip in ((2, 2, 0, True), (0, 0, 1, False), (1, 1, 2, False)):
            new[name] = adam(1, matrix, flip, factor, g1, weights[which], m[which], v[which], None)
        for name, which, matrix, flip in ((2, 2, 0, True), (0, 0, 1, False), (1, 1, 2, False)):
            new[name] = adam(0, matrix, flip, factor, g0, weights[which], m[which], v[which], new[name])
        return tuple(new[i][which] for which in range(3) for i in range(3))

    return jax.shard_map(
        step,
        mesh=mesh,
        in_specs=(P(("rep", "dp"), None, None),) * 2 + (P(None, None, None),) * 9,
        out_specs=(P("rep", None, None),) * 9,
        check_vma=False,
    )
```

time: 1040 us -> 597 us (0.57)
  Pallas kernels: 0 us -> 537 us
  waiting for transfers between devices: 514 us -> 0.07 us
  matrix products: 325 us -> 0 us
  other arithmetic: 164 us -> 1.98 us
  blocking collectives: 0 us -> 40.6 us
  local copies, waits for them, and re-layouts: 13.7 us -> 0.01 us
    pallas_call x0 -> x11, Pallas kernels: none -> 537 us  [the longest x2 212 us: reduced(): pl.pallas_call(entry(body), out_shape=(jax.ShapeDtypeStruct((total, 32, C...]
    psum x1 -> x0, waiting for transfers between devices: 514 us -> none  [step(): summed[number] = [lax.psum(by_w[name], 'dp') for name in NAMES]]
    dot_general x15 -> x0, matrix products: 325 us -> none  [the longest x5 114 us: layer(): up = jnp.dot(a, w['w_up'], preferred_element_type=jnp.float32)]
    convert_element_type x2 -> x0, other arithmetic: 123 us -> none  [adamw(): return ((w - 0.02 * step).astype(jnp.bfloat16), m, v)]
    psum x0 -> x1, blocking collectives: none -> 40.6 us  [step(): squares = lax.psum(jnp.sum(sq1) + jnp.sum(sq0), 'dp')]
    reduce_sum x4 -> x2, other arithmetic: 34.5 us -> 1.98 us  [step(): squares = lax.psum(jnp.sum(sq1) + jnp.sum(sq0), 'dp')]
    unnamed x28 -> x2, local copies, waits for them, and re-layouts: 13.7 us -> 0.01 us
  transfers between devices with their start and end apart: 1 -> 2, of which waited for: 1 -> 0; matrix products, arithmetic and copies ran while one was open for 0% -> 0% of each run, Pallas kernels for 0% -> 44%
where the time goes in v1:
time: 597 us; the launch traced here: 596 us
  Pallas kernels  537 us (90%)
  blocking collectives  40.6 us (7%)
  between operations  16.1 us (3%)
    pallas_call x2, Pallas kernels, reduced(): pl.pallas_call(entry(body), out_shape=(jax.ShapeDtypeStruct((total, 32, C...  212 us
    pallas_call x6, Pallas kernels, adam(): pl.pallas_call(functools.partial(adam_kernel, layer, matrix, per, flip),...  169 us
    pallas_call x3, Pallas kernels, row_local(): pl.pallas_call(kernel, grid=(tokens // ROWS,), in_specs=[spec(a) for a in...  156 us
    psum x1, blocking collectives, step(): squares = lax.psum(jnp.sum(sq1) + jnp.sum(sq0), 'dp')  40.6 us
  transfers between devices with their start and end apart: 2, of which 0 were waited for; matrix products, arithmetic and copies ran while one was open for 0% of the time, Pallas kernels for 44%

profile of v1, /device:TPU:0, one launch (start us, length us, event | category | flops | bytes accessed | tf_op | source)
XLA Modules:
  0.0 596.3 jit_solution(2267273229734572796)
XLA Ops:
  7.2 0.0 all-gather.7.cloned.1.call-start
  7.2 48.4 %fwd0.1 = (bf16[2048,2816]{1,0:T(8,128)(2,1)}, f32[2048,2816]{1,0:T(8,128)}, f32[2048,2816]{1,0:T(8,128)}, bf16[1024,2048]{1,0:T(8,128)(2,1)}, bf16[2048,1024]{1,0:T(8,128)(2,1)}) custom-call(bf16[1,2048,1024]{2,1,0:T(8,128)(2,1)} %x_ref.1, bf16[2,1024,2816]{2,1,0:T(8,128)(2,1)} %w_ref.7, bf16[2,1024,2816]{2,1,0:T(8,128)(2,1)} %w_ref.9, ...), custom_call_target="tpu_custom_call" | custom-call | flops 35433480192 | bytes 46137344 | tf_op jit(solution)/shard_map/fwd0/pallas_call | solution.py:122
  55.7 51.2 %top.1 = (bf16[2048,2816]{1,0:T(8,128)(2,1)}, bf16[2048,2816]{1,0:T(8,128)(2,1)}, bf16[2048,2816]{1,0:T(8,128)(2,1)}, bf16[1024,2048]{1,0:T(8,128)(2,1)}, bf16[1024,2048]{1,0:T(8,128)(2,1)}) custom-call(bf16[2048,1024]{1,0:T(8,128)(2,1)} %get-tuple-element.44.h_ref, bf16[1,2048,1024]{2,1,0:T(8,128)(2,1)} %dy_ref.3, bf16[2,1024,2816]{2,1,0:T(8,128)(2,1)} %w_ref.7, ...), custom_call_target="tpu_custom_call" | custom-call | flops 35433480192 | bytes 46137344 | tf_op jit(solution)/shard_map/top/pallas_call | solution.py:122
  106.8 89.2 %reduce1.1 = (bf16[33,32,256]{2,1,0:T(8,128)(2,1)}, f32[32,256]{1,0:T(8,128)}) custom-call(bf16[1024,2048]{1,0:T(8,128)(2,1)} %get-tuple-element.45.refs_0_, bf16[1024,2048]{1,0:T(8,128)(2,1)} %get-tuple-element.46.refs_1_, bf16[2048,2816]{1,0:T(8,128)(2,1)} %get-tuple-element.47.refs_2_, bf16[2048,2816]{1,0:T(8,128)(2,1)} %get-tuple-element.48.refs_3_.dg1_ref, ...), custom_call_target="tpu_custom_call" | custom-call | flops 35433480192 | bytes 34603008 | tf_op jit(solution)/shard_map/reduce1/pallas_call | solution.py:297
  196.0 0.0 all-gather.7.cloned.1.call-update
  196.0 0.2 all-gather.5.cloned.1.call-start
  196.3 56.6 %between.1 = (bf16[2048,2816]{1,0:T(8,128)(2,1)}, bf16[2048,2816]{1,0:T(8,128)(2,1)}, bf16[1024,2048]{1,0:T(8,128)(2,1)}) custom-call(bf16[2048,2816]{1,0:T(8,128)(2,1)} %get-tuple-element.48.refs_3_.dg1_ref, bf16[2048,2816]{1,0:T(8,128)(2,1)} %get-tuple-element.49.refs_4_.du1_ref, bf16[2048,1024]{1,0:T(8,128)(2,1)} %get-tuple-element.44.h_ref, ...), custom_call_target="tpu_custom_call" | custom-call | flops 35433480192 | bytes 46137344 | tf_op jit(solution)/shard_map/between/pallas_call | solution.py:122
  252.9 0.0 copy-start
  252.9 122.4 %reduce2.1 = (bf16[33,32,256]{2,1,0:T(8,128)(2,1)}, f32[32,256]{1,0:T(8,128)}) custom-call(bf16[1024,2048]{1,0:T(8,128)(2,1)} %get-tuple-element.53.refs_0_, bf16[1024,2048]{1,0:T(8,128)(2,1)} %get-tuple-element.54.refs_1_, bf16[2048,2816]{1,0:T(8,128)(2,1)} %get-tuple-element.55.refs_2_, bf16[2048,2816]{1,0:T(8,128)(2,1)} %get-tuple-element.56.refs_3_, ...), custom_call_target="tpu_custom_call" | custom-call | flops 35433480192 | bytes 34603008 | tf_op jit(solution)/shard_map/reduce2/pallas_call | solution.py:297
  375.3 0.0 all-gather.5.cloned.1.call-update
  375.4 1.4 reduce_sum.19
  376.7 0.0 copy-done
  376.7 0.6 reduce_sum.18
  378.6 40.6 %psum.7 = f32[]{:T(128)} all-reduce(f32[]{:T(128)S(6)} %add.8), channel_id=1, replica_groups=mesh['rep'=1,'dp'=32] {'dp'}, use_global_device_ids=true, to_apply=%region_2.0 | all-reduce | flops 1 | bytes 8 | tf_op jit(solution)/shard_map/psum | solution.py:385
  419.9 0.0 all-gather.7.cloned.1.call-done
  420.0 29.8 %adam10.1 = (bf16[2,2816,1024]{2,1,0:T(8,128)(2,1)}, f32[2,2816,1024]{2,1,0:T(8,128)}, f32[2,2816,1024]{2,1,0:T(8,128)}) custom-call(f32[1,1]{1,0:T(1,128)} %bitcast.factor_ref, bf16[32,33,32,256]{3,2,1,0:T(8,128)(2,1)} %bitcast.3, bf16[2,2816,1024]{2,1,0:T(8,128)(2,1)} %w_ref.11, f32[2,2816,1024]{2,1,0:T(8,128)} %m_ref.11, f32[2,2816,1024]{2,1,0:T(8,128)} %v_ref.11), custom_call_target="tpu_custom_call" | custom-call | flops 28835840 | bytes 63438848 | tf_op jit(solution)/shard_map/adam10/pallas_call | solution.py:355
  449.8 27.5 %adam12.1 = (bf16[2,1024,2816]{2,1,0:T(8,128)(2,1)}, f32[2,1024,2816]{2,1,0:T(8,128)}, f32[2,1024,2816]{2,1,0:T(8,128)}) custom-call(f32[1,1]{1,0:T(1,128)} %bitcast.factor_ref, bf16[32,33,32,256]{3,2,1,0:T(8,128)(2,1)} %bitcast.4, bf16[2,1024,2816]{2,1,0:T(8,128)(2,1)} %w_ref.9, f32[2,1024,2816]{2,1,0:T(8,128)} %m_ref.9, f32[2,1024,2816]{2,1,0:T(8,128)} %v_ref.9), custom_call_target="tpu_custom_call" | custom-call | flops 28835840 | bytes 63438848 | tf_op jit(solution)/shard_map/adam12/pallas_call | solution.py:355
  477.2 27.5 %adam11.1 = (bf16[2,1024,2816]{2,1,0:T(8,128)(2,1)}, f32[2,1024,2816]{2,1,0:T(8,128)}, f32[2,1024,2816]{2,1,0:T(8,128)}) custom-call(f32[1,1]{1,0:T(1,128)} %bitcast.factor_ref, bf16[32,33,32,256]{3,2,1,0:T(8,128)(2,1)} %bitcast.5, bf16[2,1024,2816]{2,1,0:T(8,128)(2,1)} %w_ref.7, f32[2,1024,2816]{2,1,0:T(8,128)} %m_ref.7, f32[2,1024,2816]{2,1,0:T(8,128)} %v_ref.7), custom_call_target="tpu_custom_call" | custom-call | flops 28835840 | bytes 63438848 | tf_op jit(solution)/shard_map/adam11/pallas_call | solution.py:355
  504.7 0.0 all-gather.5.cloned.1.call-done
  504.7 29.8 %adam00.1 = (bf16[2,2816,1024]{2,1,0:T(8,128)(2,1)}, f32[2,2816,1024]{2,1,0:T(8,128)}, f32[2,2816,1024]{2,1,0:T(8,128)}) custom-call(f32[1,1]{1,0:T(1,128)} %bitcast.factor_ref, bf16[32,33,32,256]{3,2,1,0:T(8,128)(2,1)} %bitcast.6, bf16[2,2816,1024]{2,1,0:T(8,128)(2,1)} %w_ref.11, ...), custom_call_target="tpu_custom_call", output_to_operand_aliasing={{0}: (5, {}), {1}: (6, {}), {2}: (7, {})} | custom-call | flops 28835840 | bytes 63438848 | tf_op jit(solution)/shard_map/adam00/pallas_call | solution.py:355
  534.5 27.5 %adam02.1 = (bf16[2,1024,2816]{2,1,0:T(8,128)(2,1)}, f32[2,1024,2816]{2,1,0:T(8,128)}, f32[2,1024,2816]{2,1,0:T(8,128)}) custom-call(f32[1,1]{1,0:T(1,128)} %bitcast.factor_ref, bf16[32,33,32,256]{3,2,1,0:T(8,128)(2,1)} %bitcast.7, bf16[2,1024,2816]{2,1,0:T(8,128)(2,1)} %w_ref.9, ...), custom_call_target="tpu_custom_call", output_to_operand_aliasing={{0}: (5, {}), {1}: (6, {}), {2}: (7, {})} | custom-call | flops 28835840 | bytes 63438848 | tf_op jit(solution)/shard_map/adam02/pallas_call | solution.py:355
  561.9 27.5 %adam01.1 = (bf16[2,1024,2816]{2,1,0:T(8,128)(2,1)}, f32[2,1024,2816]{2,1,0:T(8,128)}, f32[2,1024,2816]{2,1,0:T(8,128)}) custom-call(f32[1,1]{1,0:T(1,128)} %bitcast.factor_ref, bf16[32,33,32,256]{3,2,1,0:T(8,128)(2,1)} %bitcast.8, bf16[2,1024,2816]{2,1,0:T(8,128)(2,1)} %w_ref.7, ...), custom_call_target="tpu_custom_call", output_to_operand_aliasing={{0}: (5, {}), {1}: (6, {}), {2}: (7, {})} | custom-call | flops 28835840 | bytes 63438848 | tf_op jit(solution)/shard_map/adam01/pallas_call | solution.py:355
Async XLA Ops:
  7.2 412.8 %all-gather.7.cloned.1.call-start = ((), (), s32[]{:S(2)}) async-start(), calls=%async_computation.1 | async-start | bytes 17842176 | tf_op jit(solution)/shard_map/all_gather | solution.py:388
  196.0 308.6 %all-gather.5.cloned.1.call-start = ((), (), s32[]{:S(2)}) async-start(), calls=%async_computation | async-start | bytes 17842176 | tf_op jit(solution)/shard_map/all_gather | solution.py:389
  252.9 123.8 %copy-start = (f32[32,256]{1,0:T(8,128)S(1)}, f32[32,256]{1,0:T(8,128)}, u32[]{:S(2)}) copy-start(f32[32,256]{1,0:T(8,128)} %get-tuple-element.50) | copy-start | bytes 98308
Sparse Core Ops, SparseCore 0:
  196.2 154.8 all-gather.6
  375.5 116.3 all-gather.4
